TPU v7x, 32 devices: a whole 2x2x4 slice. The times are simulated.
32 devices in a mesh: high: 4 (over z), low: 2 (over x), unit: 4 (over y, core).
Axes of the slice: x: 2, y: 2, z: 4, core: 2. Of those that a mesh axis runs over, the one named last changes fastest.
Arguments:
- wave_parts: float32 [8, 32, 128, 128], P('unit', ('high', 'low')), parts along dimension 0, may hold values from -6 to 6
- level_table: float32 [128, 128, 128], P(('unit', 'high', 'low')), parts along dimension 0, may hold values from -2 to 2
- phase_angles: float32 [8, 128], P('unit'), parts along dimension 0, may hold values from 0.3 to 1.2
- mix_angles: float32 [8, 4], P('unit'), parts along dimension 0, may hold values from 0.3 to 1.2
Outputs:
- result_parts: float32 [8, 32, 128, 128], P('unit', ('high', 'low')), parts along dimension 0
There are 4 independent parts, one for each index of `unit`. A program takes and returns all parts, laid end to end along the dimension named above; each array names one. Nothing has to cross between parts.
All inputs are finite; a program needn't handle non-finite values.
Results may differ from a plain program's by a relative error of at most 0.0003.
Values sent between devices are 32-bit elements.
A program may use at most 64 MiB of HBM per device.

v0:
```python
import jax
import jax.numpy as jnp
from jax import lax
from jax.sharding import PartitionSpec as P

LAYERS = 2


def partner(value, axis, bit):
    mask = 2**bit
    pairs = [(source, source ^ mask) for source in range(lax.axis_size(axis))]
    return lax.ppermute(value, axis, pairs)


def count_bits(values, count):
    places = jnp.arange(count.bit_length() - 1, dtype=jnp.int32)
    return jnp.sum(values[..., None] >> places & 1, axis=-1)


def mix_table(count, angle):
    rank = jnp.arange(count, dtype=jnp.int32)
    apart = count_bits(rank[:, None] ^ rank[None, :], count)
    bits = count.bit_length() - 1
    size = jnp.cos(angle) ** (bits - apart).astype(jnp.float32) * jnp.sin(angle) ** apart.astype(
        jnp.float32
    )
    real_sign = jnp.where(apart % 4 == 0, 1.0, jnp.where(apart % 4 == 2, -1.0, 0.0)).astype(
        jnp.float32
    )
    imag_sign = jnp.where(apart % 4 == 1, -1.0, jnp.where(apart % 4 == 3, 1.0, 0.0)).astype(
        jnp.float32
    )
    return (size * real_sign, size * imag_sign)


def turn_dim(values, dim, angle):
    real_part, imag_part = mix_table(values.shape[dim], angle)

    def times(table):
        moved = jnp.tensordot(values, table, axes=([dim], [0]), precision=lax.Precision.HIGHEST)
        return jnp.moveaxis(moved, -1, dim)

    by_real = times(real_part)
    by_imag = times(imag_part)
    return jnp.stack([by_real[0] - by_imag[1], by_real[1] + by_imag[0]])


def turn_phase(values, levels, angle):
    turn = angle * levels
    return jnp.stack(
        [
            values[0] * jnp.cos(turn) + values[1] * jnp.sin(turn),
            values[1] * jnp.cos(turn) - values[0] * jnp.sin(turn),
        ]
    )


def body(wave_parts, level_table, phase_angles, mix_angles):
    values = wave_parts
    for layer in range(LAYERS):
        values = turn_phase(values, level_table, phase_angles[layer])
        values = turn_dim(values, 3, mix_angles[layer, 0])
        values = turn_dim(values, 2, mix_angles[layer, 1])
        values = turn_dim(values, 1, mix_angles[layer, 2])
        for bit in range(lax.axis_size("high").bit_length() - 1):
            other = partner(values, "high", bit)
            angle = mix_angles[layer, 2]
            real_new = jnp.cos(angle) * values[0] + jnp.sin(angle) * other[1]
            imag_new = jnp.cos(angle) * values[1] - jnp.sin(angle) * other[0]
            values = jnp.stack([real_new, imag_new])
        for bit in range(lax.axis_size("low").bit_length() - 1):
            other = partner(values, "low", bit)
            angle = mix_angles[layer, 3]
            real_new = jnp.cos(angle) * values[0] + jnp.sin(angle) * other[1]
            imag_new = jnp.cos(angle) * values[1] - jnp.sin(angle) * other[0]
            values = jnp.stack([real_new, imag_new])
    return values


def solution(mesh):
    placed = (
        P("unit", ("high", "low"), None, None),
        P(("unit", "high", "low"), None, None),
        P("unit", None),
        P("unit", None),
    )
    return jax.shard_map(
        body,
        mesh=mesh,
        in_specs=placed,
        out_specs=P("unit", ("high", "low"), None, None),
        check_vma=False,
    )
```

profile of v0, /device:TPU:0, one launch (start us, length us, event | category | flops | bytes accessed | tf_op | source)
XLA Modules:
  0.0 129.5 jit_solution(8729161817234570019)
XLA Ops:
  2.8 2.1 %fusion.21 = (f32[1,4,128,128]{3,2,1,0:T(8,128)S(1)}, f32[1,4,128,128]{3,2,1,0:T(8,128)S(1)}) fusion(f32[2,4,128,128]{3,2,1,0:T(8,128)} %param.4, f32[4,128,128]{2,1,0:T(8,128)} %param.5, f32[128]{0:T(128)S(1)} %get-tuple-element.44), kind=kLoop, calls=%fused_computation.69 | loop fusion | flops 458752 | bytes 1311232 | tf_op jit(solution)/shard_map/stack | solution.py:50
  8.0 1.1 convolution_bitcast_fusion.6
  9.1 1.1 convolution_bitcast_fusion.7
  12.0 1.1 convolution_bitcast_fusion.4
  13.1 1.1 convolution_bitcast_fusion.5
  14.4 3.1 %collective-permute-start = (f32[2,4,128,128]{3,1,2,0:T(4,128)S(1)}, f32[2,4,128,128]{3,1,2,0:T(4,128)S(1)}, u32[]{:S(2)}, u32[]{:S(2)}) collective-permute-start(f32[2,4,128,128]{3,1,2,0:T(4,128)S(1)} %pad_maximum_fusion.3), channel_id=1, source_target_pairs={{0,8},{8,0},{16,24},{24,16},{1,9},{9,1},{17,25},{25,17},{2,10},{10... | collective-permute-start | bytes 1572872 | tf_op jit(solution)/shard_map/ppermute | solution.py:12
  17.5 11.9 %collective-permute-done = f32[2,4,128,128]{3,1,2,0:T(4,128)S(1)} collective-permute-done((f32[2,4,128,128]{3,1,2,0:T(4,128)S(1)}, f32[2,4,128,128]{3,1,2,0:T(4,128)S(1)}, u32[]{:S(2)}, u32[]{:S(2)}) %collective-permute-start) | collective-permute-done | bytes 524320 | tf_op jit(solution)/shard_map/ppermute | solution.py:12
  29.7 2.8 %collective-permute-start.1 = (f32[2,4,128,128]{3,1,2,0:T(4,128)S(1)}, f32[2,4,128,128]{3,1,2,0:T(4,128)S(1)}, u32[]{:S(2)}, u32[]{:S(2)}) collective-permute-start(f32[2,4,128,128]{3,1,2,0:T(4,128)S(1)} %pad_maximum_fusion.4), channel_id=1, source_target_pairs={{0,16},{8,24},{16,0},{24,8},{1,17},{9,25},{17,1},{25,9},{2,18},{10... | collective-permute-start | bytes 1572872 | tf_op jit(solution)/shard_map/ppermute | solution.py:12
  32.6 22.5 %collective-permute-done.1 = f32[2,4,128,128]{3,1,2,0:T(4,128)S(1)} collective-permute-done((f32[2,4,128,128]{3,1,2,0:T(4,128)S(1)}, f32[2,4,128,128]{3,1,2,0:T(4,128)S(1)}, u32[]{:S(2)}, u32[]{:S(2)}) %collective-permute-start.1) | collective-permute-done | bytes 524320 | tf_op jit(solution)/shard_map/ppermute | solution.py:12
  55.3 1.4 %collective-permute-start.2 = (f32[2,4,128,128]{3,1,2,0:T(4,128)S(1)}, f32[2,4,128,128]{3,1,2,0:T(4,128)S(1)}, u32[]{:S(2)}, u32[]{:S(2)}) collective-permute-start(f32[2,4,128,128]{3,1,2,0:T(4,128)S(1)} %pad_maximum_fusion.5), channel_id=1, source_target_pairs={{0,4},{4,0},{1,5},{5,1},{2,6},{6,2},{3,7},{7,3},{8,12},{12,8},{9,1... | collective-permute-start | bytes 1572872 | tf_op jit(solution)/shard_map/ppermute | solution.py:12
  62.2 6.1 %collective-permute-done.2 = f32[2,4,128,128]{3,1,2,0:T(4,128)S(1)} collective-permute-done((f32[2,4,128,128]{3,1,2,0:T(4,128)S(1)}, f32[2,4,128,128]{3,1,2,0:T(4,128)S(1)}, u32[]{:S(2)}, u32[]{:S(2)}) %collective-permute-start.2) | collective-permute-done | bytes 524320 | tf_op jit(solution)/shard_map/ppermute | solution.py:12
  68.3 2.4 %add_bitcast_fusion = (f32[1,4,128,128]{3,1,2,0:T(4,128)S(1)}, f32[1,4,128,128]{3,1,2,0:T(4,128)S(1)}) fusion(f32[4,128,128]{2,1,0:T(8,128)S(1)} %copy-done, f32[128]{0:T(128)S(1)} %get-tuple-element.45, f32[2,4,128,128]{3,1,2,0:T(4,128)S(1)} %collective-permute-done.2, f32[]{:T(128)} %bitcast.28, f32[1,4,128,128]{3,1,2,0:T(4,128)S(1)} %get-tuple-element.29, ...), kind=kLoop, calls=%fused_computation.76 | loop fusion | flops 851968 | bytes 1835528 | tf_op jit(solution)/shard_map/stack | solution.py:50
  70.8 0.8 fusion
  72.4 1.1 convolution_bitcast_fusion.2
  73.5 1.1 convolution_bitcast_fusion.3
  75.0 1.1 convolution_bitcast_fusion
  76.0 1.1 convolution_bitcast_fusion.1
  77.4 1.3 collective-permute-start.3
  78.7 11.0 %collective-permute-done.3 = f32[2,4,128,128]{3,1,2,0:T(4,128)S(1)} collective-permute-done((f32[2,4,128,128]{3,1,2,0:T(4,128)S(1)}, f32[2,4,128,128]{3,1,2,0:T(4,128)S(1)}, u32[]{:S(2)}, u32[]{:S(2)}) %collective-permute-start.3) | collective-permute-done | bytes 524320 | tf_op jit(solution)/shard_map/ppermute | solution.py:12
  90.0 3.5 %collective-permute-start.4 = (f32[2,4,128,128]{3,1,2,0:T(4,128)S(1)}, f32[2,4,128,128]{3,1,2,0:T(4,128)S(1)}, u32[]{:S(2)}, u32[]{:S(2)}) collective-permute-start(f32[2,4,128,128]{3,1,2,0:T(4,128)S(1)} %pad_maximum_fusion.10), channel_id=1, source_target_pairs={{0,16},{8,24},{16,0},{24,8},{1,17},{9,25},{17,1},{25,9},{2,18},{10... | collective-permute-start | bytes 1572872 | tf_op jit(solution)/shard_map/ppermute | solution.py:12
  93.4 21.7 %collective-permute-done.4 = f32[2,4,128,128]{3,1,2,0:T(4,128)S(1)} collective-permute-done((f32[2,4,128,128]{3,1,2,0:T(4,128)S(1)}, f32[2,4,128,128]{3,1,2,0:T(4,128)S(1)}, u32[]{:S(2)}, u32[]{:S(2)}) %collective-permute-start.4) | collective-permute-done | bytes 524320 | tf_op jit(solution)/shard_map/ppermute | solution.py:12
  115.4 1.6 %collective-permute-start.5 = (f32[2,4,128,128]{3,1,2,0:T(4,128)S(1)}, f32[2,4,128,128]{3,1,2,0:T(4,128)S(1)}, u32[]{:S(2)}, u32[]{:S(2)}) collective-permute-start(f32[2,4,128,128]{3,1,2,0:T(4,128)S(1)} %pad_maximum_fusion.11), channel_id=1, source_target_pairs={{0,4},{4,0},{1,5},{5,1},{2,6},{6,2},{3,7},{7,3},{8,12},{12,8},{9,1... | collective-permute-start | bytes 1572872 | tf_op jit(solution)/shard_map/ppermute | solution.py:12
  118.4 10.0 %collective-permute-done.5 = f32[2,4,128,128]{3,1,2,0:T(4,128)S(1)} collective-permute-done((f32[2,4,128,128]{3,1,2,0:T(4,128)S(1)}, f32[2,4,128,128]{3,1,2,0:T(4,128)S(1)}, u32[]{:S(2)}, u32[]{:S(2)}) %collective-permute-start.5) | collective-permute-done | bytes 524320 | tf_op jit(solution)/shard_map/ppermute | solution.py:12
  128.7 0.8 copy.32
  (40 shorter events, 6.4 us)
Async XLA Ops:
  0.0 0.7 copy-start.1
  2.0 0.7 copy-start.2
  14.4 15.1 %collective-permute-start = (f32[2,4,128,128]{3,1,2,0:T(4,128)S(1)}, f32[2,4,128,128]{3,1,2,0:T(4,128)S(1)}, u32[]{:S(2)}, u32[]{:S(2)}) collective-permute-start(f32[2,4,128,128]{3,1,2,0:T(4,128)S(1)} %pad_maximum_fusion.3), channel_id=1, source_target_pairs={{0,8},{8,0},{16,24},{24,16},{1,9},{9,1},{17,25},{25,17},{2,10},{10... | collective-permute-start | bytes 1572872 | tf_op jit(solution)/shard_map/ppermute | solution.py:12
  29.7 25.3 %collective-permute-start.1 = (f32[2,4,128,128]{3,1,2,0:T(4,128)S(1)}, f32[2,4,128,128]{3,1,2,0:T(4,128)S(1)}, u32[]{:S(2)}, u32[]{:S(2)}) collective-permute-start(f32[2,4,128,128]{3,1,2,0:T(4,128)S(1)} %pad_maximum_fusion.4), channel_id=1, source_target_pairs={{0,16},{8,24},{16,0},{24,8},{1,17},{9,25},{17,1},{25,9},{2,18},{10... | collective-permute-start | bytes 1572872 | tf_op jit(solution)/shard_map/ppermute | solution.py:12
  55.1 13.1 %copy-start = (f32[4,128,128]{2,1,0:T(8,128)S(1)}, f32[4,128,128]{2,1,0:T(8,128)}, u32[]{:S(2)}) copy-start(f32[4,128,128]{2,1,0:T(8,128)} %param.5) | copy-start | bytes 786436
  55.3 13.0 %collective-permute-start.2 = (f32[2,4,128,128]{3,1,2,0:T(4,128)S(1)}, f32[2,4,128,128]{3,1,2,0:T(4,128)S(1)}, u32[]{:S(2)}, u32[]{:S(2)}) collective-permute-start(f32[2,4,128,128]{3,1,2,0:T(4,128)S(1)} %pad_maximum_fusion.5), channel_id=1, source_target_pairs={{0,4},{4,0},{1,5},{5,1},{2,6},{6,2},{3,7},{7,3},{8,12},{12,8},{9,1... | collective-permute-start | bytes 1572872 | tf_op jit(solution)/shard_map/ppermute | solution.py:12
  77.4 12.3 %collective-permute-start.3 = (f32[2,4,128,128]{3,1,2,0:T(4,128)S(1)}, f32[2,4,128,128]{3,1,2,0:T(4,128)S(1)}, u32[]{:S(2)}, u32[]{:S(2)}) collective-permute-start(f32[2,4,128,128]{3,1,2,0:T(4,128)S(1)} %pad_maximum_fusion.9), channel_id=1, source_target_pairs={{0,8},{8,0},{16,24},{24,16},{1,9},{9,1},{17,25},{25,17},{2,10},{10... | collective-permute-start | bytes 1572872 | tf_op jit(solution)/shard_map/ppermute | solution.py:12
  90.0 25.2 %collective-permute-start.4 = (f32[2,4,128,128]{3,1,2,0:T(4,128)S(1)}, f32[2,4,128,128]{3,1,2,0:T(4,128)S(1)}, u32[]{:S(2)}, u32[]{:S(2)}) collective-permute-start(f32[2,4,128,128]{3,1,2,0:T(4,128)S(1)} %pad_maximum_fusion.10), channel_id=1, source_target_pairs={{0,16},{8,24},{16,0},{24,8},{1,17},{9,25},{17,1},{25,9},{2,18},{10... | collective-permute-start | bytes 1572872 | tf_op jit(solution)/shard_map/ppermute | solution.py:12
  115.4 13.0 %collective-permute-start.5 = (f32[2,4,128,128]{3,1,2,0:T(4,128)S(1)}, f32[2,4,128,128]{3,1,2,0:T(4,128)S(1)}, u32[]{:S(2)}, u32[]{:S(2)}) collective-permute-start(f32[2,4,128,128]{3,1,2,0:T(4,128)S(1)} %pad_maximum_fusion.11), channel_id=1, source_target_pairs={{0,4},{4,0},{1,5},{5,1},{2,6},{6,2},{3,7},{7,3},{8,12},{12,8},{9,1... | collective-permute-start | bytes 1572872 | tf_op jit(solution)/shard_map/ppermute | solution.py:12
where the time goes:
time: 130 us; the launch traced here: 129 us
  waiting for transfers between devices  83.2 us (64%)
  starting transfers between devices  13.7 us (11%)
  matrix products  11.7 us (9%)
  between operations  11.5 us (9%)
  other arithmetic  6.71 us (5%)
  local copies, waits for them, and re-layouts  2.65 us (2%)
    ppermute x6, waiting for transfers between devices, partner(): return lax.ppermute(value, axis, pairs)  83.2 us
    ppermute x6, starting transfers between devices, partner(): return lax.ppermute(value, axis, pairs)  13.7 us
    dot_general x12, matrix products, times(): jnp.tensordot(values, table, axes=([dim], [0]), precision=lax.Precision.H...  11.7 us
    another operation x3, other arithmetic, turn_phase(): jnp.stack([values[0] * jnp.cos(turn) + values[1] * jnp.sin(turn), values[...  4.54 us
  transfers between devices with their start and end apart: 6, of which 6 were waited for; matrix products, arithmetic and copies ran while one was open for 0% of the time, Pallas kernels for 0%

commit v1 on v0

v1 whole, which is shorter than its diff:
```python
import functools
import math

import jax
import jax.numpy as jnp
from jax import lax
from jax.experimental import pallas as pl
from jax.experimental.pallas import tpu as pltpu
from jax.sharding import PartitionSpec as P

LAYERS = 2
MESH = pl.DeviceIdType.MESH
CHUNKS = 4


def cos_sin(x):
    turns = jnp.floor(x * (0.5 / math.pi) + 0.5)
    r = x - turns * 6.28125
    r = r - turns * (2 * math.pi - 6.28125)
    y = r * r
    sine = jnp.full_like(y, -1.0 / math.factorial(19))
    for n in range(17, 0, -2):
        sine = sine * y + (-1.0) ** (n // 2) / math.factorial(n)
    cosine = jnp.full_like(y, -1.0 / math.factorial(18))
    for n in range(16, -1, -2):
        cosine = cosine * y + (-1.0) ** (n // 2) / math.factorial(n)
    return cosine, sine * r


def bits_of(count):
    return count.bit_length() - 1


def popcount(values, bits):
    total = values & 1
    for k in range(1, bits):
        total = total + ((values >> k) & 1)
    return total


def rotation(size, c, s, transposed):
    out = lax.broadcasted_iota(jnp.int32, (size, size), 1 if transposed else 0)
    inn = lax.broadcasted_iota(jnp.int32, (size, size), 0 if transposed else 1)
    differ = out ^ inn
    c = jnp.broadcast_to(c, (size, size))
    s = jnp.broadcast_to(s, (size, size))
    table = None
    for k in range(bits_of(size)):
        turned = jnp.where(((out >> k) & 1) == 1, -s, s)
        factor = jnp.where(((differ >> k) & 1) == 1, turned, c)
        table = factor if table is None else table * factor
    return table


def rotate_list(parts, bit, c, s):
    fresh = list(parts)
    for n in range(len(parts)):
        if not n >> bit & 1:
            m = n | 1 << bit
            fresh[n] = c * parts[n] + s * parts[m]
            fresh[m] = c * parts[m] - s * parts[n]
    return fresh


def mm(a, b):
    return lax.dot_general(
        a,
        b,
        (((1,), (0,)), ((), ())),
        precision=lax.Precision.HIGHEST,
        preferred_element_type=jnp.float32,
    )


def kernel(
    n_high,
    n_low,
    blocks,
    rows,
    chunks,
    wave,
    level,
    phase,
    mix,
    out,
    lane_tab,
    row_tab,
    work,
    s1,
    r1,
    s2,
    r2,
    lv,
    trig,
    send_lv,
    recv_lv,
    send1,
    recv1,
    send2,
    recv2,
):
    group = n_high * n_low
    lanes = wave.shape[-1]
    total = blocks * rows
    piece = total // group
    rc = piece // chunks
    me = lax.axis_index("high") * n_low + lax.axis_index("low")

    def peer(k):
        return lax.rem(me + k, group)

    def where_is(other):
        return {"high": other // n_low, "low": lax.rem(other, n_low)}

    barrier = pltpu.get_barrier_semaphore()
    for k in range(1, group):
        pl.semaphore_signal(barrier, inc=1, device_id=where_is(peer(k)), device_id_type=MESH)

    mix_c, mix_s = cos_sin(mix[...])

    def angle(layer, g):
        return mix_c[layer : layer + 1, g : g + 1], mix_s[layer : layer + 1, g : g + 1]

    pl.semaphore_wait(barrier, group - 1)

    def level_copy(k):
        other = peer(k)
        return pltpu.make_async_remote_copy(
            src_ref=level.at[pl.ds(pl.multiple_of(other * piece, piece), piece)],
            dst_ref=lv.at[me],
            send_sem=send_lv.at[k],
            recv_sem=recv_lv.at[me],
            device_id=where_is(other),
            device_id_type=MESH,
        )

    def part_copy(source, target, send, recv, c, k):
        other = peer(k)
        return pltpu.make_async_remote_copy(
            src_ref=source.at[c, other],
            dst_ref=target.at[c, me],
            send_sem=send.at[c, k],
            recv_sem=recv.at[c, me],
            device_id=where_is(other),
            device_id_type=MESH,
        )

    def arrived(ref, sem, k):
        return pltpu.make_async_remote_copy(
            src_ref=ref,
            dst_ref=ref,
            send_sem=send_lv.at[k],
            recv_sem=sem,
            device_id=where_is(peer(k)),
            device_id_type=MESH,
        )

    for k in range(1, group):
        level_copy(k).start()

    for layer in range(LAYERS):
        lane_tab[layer] = rotation(lanes, *angle(layer, 0), True)
        row_tab[layer] = rotation(rows, *angle(layer, 1), False)

    step = min(16, rows)
    own_bits = popcount(me, bits_of(group))

    def quarter(row_start, count, block):
        row = lax.broadcasted_iota(jnp.int32, (count, lanes), 0) + row_start
        lane = lax.broadcasted_iota(jnp.int32, (count, lanes), 1)
        fixed = own_bits + block.bit_count()
        return (popcount(row, bits_of(rows)) + popcount(lane, bits_of(lanes)) + fixed) & 3

    def signs(q):
        one = jnp.float32(1.0)
        first = jnp.where((q == 1) | (q == 2), -one, one)
        second = jnp.where(q >= 2, -one, one)
        return (q & 1) == 1, first, second

    @pl.loop(0, rows // step)
    def _(n):
        start = pl.multiple_of(n * step, step)
        real, imag = [], []
        for b in range(blocks):
            at = pl.ds(b * rows + start, step)
            c, s = cos_sin(phase[0:1, :] * level[at, :])
            odd, first, second = signs(quarter(start, step, b))
            c, s = jnp.where(odd, s, c) * first, jnp.where(odd, c, s) * second
            u, v = wave[0, at, :], wave[1, at, :]
            real.append(u * c + v * s)
            imag.append(v * c - u * s)
        for bit in range(bits_of(blocks)):
            real = rotate_list(real, bit, *angle(0, 2))
            imag = rotate_list(imag, bit, *angle(0, 2))
        for b in range(blocks):
            at = pl.ds(b * rows + start, step)
            work[0, at, :] = real[b]
            work[1, at, :] = imag[b]

    lv[me] = level[pl.ds(pl.multiple_of(me * piece, piece), piece), :]

    per_block = rows // piece if piece <= rows else 0
    for part in range(2):
        for b in range(blocks):
            turned = mm(work[part, b * rows : (b + 1) * rows, :], lane_tab[0])
            turned = mm(row_tab[0], turned)
            for n in range(per_block):
                for c in range(chunks):
                    at = n * piece + c * rc
                    s1[c, b * per_block + n, part] = turned[at : at + rc]

    for c in range(chunks):
        r1[c, me] = s1[c, me]
        for k in range(1, group):
            part_copy(s1, r1, send1, recv1, c, k).start()

    for k in range(1, group):
        arrived(lv.at[peer(k)], recv_lv.at[peer(k)], k).wait_recv()

    @pl.loop(0, group)
    def _(g):
        c, s = cos_sin(phase[1:2, :] * lv[g])
        trig[0, g] = c
        trig[1, g] = s

    low_bits, all_bits = bits_of(n_low), bits_of(group)
    for c in range(chunks):
        for k in range(1, group):
            arrived(r1.at[c, peer(k)], recv1.at[c, peer(k)], k).wait_recv()

        @pl.loop(0, rc // 8)
        def _(n):
            at = pl.ds(pl.multiple_of(n * 8, 8), 8)
            from_piece = pl.ds(pl.multiple_of(c * rc + n * 8, 8), 8)
            real = [r1[c, g, 0, at, :] for g in range(group)]
            imag = [r1[c, g, 1, at, :] for g in range(group)]
            for bit in range(all_bits):
                turn = angle(0, 3 if bit < low_bits else 2)
                real = rotate_list(real, bit, *turn)
                imag = rotate_list(imag, bit, *turn)
            for g in range(group):
                co, si = trig[0, g, from_piece, :], trig[1, g, from_piece, :]
                u, v = real[g], imag[g]
                real[g] = u * co + v * si
                imag[g] = v * co - u * si
            for bit in range(all_bits):
                turn = angle(1, 3 if bit < low_bits else 2)
                real = rotate_list(real, bit, *turn)
                imag = rotate_list(imag, bit, *turn)
            for g in range(group):
                s2[c, g, 0, at, :] = real[g]
                s2[c, g, 1, at, :] = imag[g]

        r2[c, me] = s2[c, me]
        for k in range(1, group):
            part_copy(s2, r2, send2, recv2, c, k).start()

    for c in range(chunks):
        for k in range(1, group):
            arrived(r2.at[c, peer(k)], recv2.at[c, peer(k)], k).wait_recv()
        turned = mm(r2[c].reshape(group * 2 * rc, lanes), lane_tab[1])
        turned = turned.reshape(group, 2, rc, lanes)
        for g in range(group):
            for part in range(2):
                at = g * piece + c * rc
                work[part, at : at + rc, :] = turned[g, part]

    for part in range(2):
        for b in range(blocks):
            at = slice(b * rows, (b + 1) * rows)
            work[part, at, :] = mm(row_tab[1], work[part, at, :])

    @pl.loop(0, rows // step)
    def _(n):
        start = pl.multiple_of(n * step, step)
        spots = [pl.ds(b * rows + start, step) for b in range(blocks)]
        real = [work[0, at, :] for at in spots]
        imag = [work[1, at, :] for at in spots]
        for bit in range(bits_of(blocks)):
            real = rotate_list(real, bit, *angle(1, 2))
            imag = rotate_list(imag, bit, *angle(1, 2))
        for b in range(blocks):
            odd, first, second = signs(quarter(start, step, b))
            out[0, spots[b], :] = jnp.where(odd, imag[b], real[b]) * first
            out[1, spots[b], :] = jnp.where(odd, real[b], imag[b]) * second

    for k in range(1, group):
        level_copy(k).wait_send()
        for c in range(chunks):
            part_copy(s1, r1, send1, recv1, c, k).wait_send()
            part_copy(s2, r2, send2, recv2, c, k).wait_send()


def body(wave_parts, level_table, phase_angles, mix_angles):
    n_high, n_low = lax.axis_size("high"), lax.axis_size("low")
    group = n_high * n_low
    _, blocks, rows, lanes = wave_parts.shape
    total = blocks * rows
    piece = total // group
    chunks = max(1, min(CHUNKS, piece // 8))
    rc = piece // chunks
    parts = pltpu.VMEM((chunks, group, 2, rc, lanes), jnp.float32)
    vmem = pl.BlockSpec(memory_space=pltpu.VMEM)
    result = pl.pallas_call(
        functools.partial(kernel, n_high, n_low, blocks, rows, chunks),
        out_shape=jax.ShapeDtypeStruct((2, total, lanes), jnp.float32),
        in_specs=[vmem] * 4,
        out_specs=vmem,
        scratch_shapes=[
            pltpu.VMEM((LAYERS, lanes, lanes), jnp.float32),
            pltpu.VMEM((LAYERS, rows, rows), jnp.float32),
            pltpu.VMEM((2, total, lanes), jnp.float32),
            parts,
            parts,
            parts,
            parts,
            pltpu.VMEM((group, piece, lanes), jnp.float32),
            pltpu.VMEM((2, group, piece, lanes), jnp.float32),
            pltpu.SemaphoreType.DMA((group,)),
            pltpu.SemaphoreType.DMA((group,)),
            pltpu.SemaphoreType.DMA((chunks, group)),
            pltpu.SemaphoreType.DMA((chunks, group)),
            pltpu.SemaphoreType.DMA((chunks, group)),
            pltpu.SemaphoreType.DMA((chunks, group)),
        ],
        compiler_params=pltpu.CompilerParams(collective_id=0, has_side_effects=True),
    )(
        wave_parts.reshape(2, total, lanes),
        level_table.reshape(total, lanes),
        phase_angles,
        mix_angles,
    )
    return result.reshape(wave_parts.shape)


def solution(mesh):
    placed = (
        P("unit", ("high", "low"), None, None),
        P(("unit", "high", "low"), None, None),
        P("unit", None),
        P("unit", None),
    )
    return jax.shard_map(
        body,
        mesh=mesh,
        in_specs=placed,
        out_specs=P("unit", ("high", "low"), None, None),
        check_vma=False,
    )
```

time: 130 us -> 45.5 us (0.35)
  waiting for transfers between devices: 83.2 us -> 0 us
  Pallas kernels: 0 us -> 43.4 us
  starting transfers between devices: 13.7 us -> 0 us
  matrix products: 11.7 us -> 0 us
  between operations: 11.5 us -> 0.01 us
  other arithmetic: 6.71 us -> 0 us
    ppermute x6 -> x0, waiting for transfers between devices: 83.2 us -> none  [partner(): return lax.ppermute(value, axis, pairs)]
    pallas_call x0 -> x1, Pallas kernels: none -> 43.4 us  [body(): pl.pallas_call(functools.partial(kernel, n_high, n_low, blocks, rows, chu...]
    ppermute x6 -> x0, starting transfers between devices: 13.7 us -> none  [partner(): return lax.ppermute(value, axis, pairs)]
    dot_general x12 -> x0, matrix products: 11.7 us -> none  [times(): jnp.tensordot(values, table, axes=([dim], [0]), precision=lax.Precision.H...]
    another operation x12 -> x0, other arithmetic: 5.42 us -> none  [the longest x3 4.54 us: turn_phase(): jnp.stack([values[0] * jnp.cos(turn) + values[1] * jnp.sin(turn), values[...]
  transfers between devices with their start and end apart: 6 -> 0, of which waited for: 6 -> 0; matrix products, arithmetic and copies ran while one was open for 0% -> 0% of each run, Pallas kernels for 0% -> 0%
where the time goes in v1:
time: 45.5 us; the launch traced here: 45.3 us
  Pallas kernels  43.4 us (95%)
  local copies, waits for them, and re-layouts  1.87 us (4%)
    pallas_call x1, Pallas kernels, body(): pl.pallas_call(functools.partial(kernel, n_high, n_low, blocks, rows, chu...  43.4 us
    unnamed x1, local copies, waits for them, and re-layouts  1.87 us

profile of v1, /device:TPU:0, one launch (start us, length us, event | category | flops | bytes accessed | tf_op | source)
XLA Modules:
  0.0 45.3 jit_solution(15711377457181093309)
XLA Ops:
  0.0 43.4 %shard_map.46 = f32[2,512,128]{2,1,0:T(8,128)} custom-call(f32[2,512,128]{2,1,0:T(8,128)} %bitcast.4, f32[512,128]{1,0:T(8,128)} %bitcast.5, f32[2,128]{1,0:T(2,128)} %phase.1, f32[2,4]{1,0:T(2,128)} %mix.1), custom_call_target="tpu_custom_call" | custom-call | tf_op jit(solution)/shard_map/pallas_call | solution.py:304
  43.4 1.9 %copy.6 = f32[2,4,128,128]{3,2,1,0:T(8,128)} copy(f32[2,4,128,128]{3,2,1,0:T(8,128)} %bitcast.3) | data formatting | bytes 1048576

commit v2 on v1

--- a/solution.py
+++ b/solution.py
@@ -62,14 +62,33 @@
     return fresh
 
 
-def mm(a, b):
-    return lax.dot_general(
-        a,
-        b,
-        (((1,), (0,)), ((), ())),
-        precision=lax.Precision.HIGHEST,
-        preferred_element_type=jnp.float32,
-    )
+def halves(values):
+    high = values.astype(jnp.bfloat16)
+    return high, (values - high.astype(jnp.float32)).astype(jnp.bfloat16)
+
+
+def lane_table(table):
+    pair = jnp.concatenate(halves(table), axis=1)
+    return jnp.concatenate([pair, pair], axis=0)
+
+
+def row_table(table):
+    pair = jnp.concatenate(halves(table), axis=0)
+    return jnp.concatenate([pair, pair], axis=1)
+
+
+def by_lane(values, table):
+    wide = jnp.concatenate(halves(values), axis=1)
+    sums = jnp.dot(wide, table, preferred_element_type=jnp.float32)
+    lanes = values.shape[1]
+    return sums[:, :lanes] + sums[:, lanes:]
+
+
+def by_row(table, values):
+    tall = jnp.concatenate(halves(values), axis=0)
+    sums = jnp.dot(table, tall, preferred_element_type=jnp.float32)
+    rows = values.shape[0]
+    return sums[:rows] + sums[rows:]
 
 
 def kernel(
@@ -86,6 +105,7 @@
     lane_tab,
     row_tab,
     work,
+    mid,
     s1,
     r1,
     s2,
@@ -159,8 +179,8 @@
         level_copy(k).start()
 
     for layer in range(LAYERS):
-        lane_tab[layer] = rotation(lanes, *angle(layer, 0), True)
-        row_tab[layer] = rotation(rows, *angle(layer, 1), False)
+        lane_tab[layer] = lane_table(rotation(lanes, *angle(layer, 0), True))
+        row_tab[layer] = row_table(rotation(rows, *angle(layer, 1), False))
 
     step = min(16, rows)
     own_bits = popcount(me, bits_of(group))
@@ -200,14 +220,16 @@
     lv[me] = level[pl.ds(pl.multiple_of(me * piece, piece), piece), :]
 
     per_block = rows // piece if piece <= rows else 0
-    for part in range(2):
-        for b in range(blocks):
-            turned = mm(work[part, b * rows : (b + 1) * rows, :], lane_tab[0])
-            turned = mm(row_tab[0], turned)
+    for b in range(blocks):
+        at = slice(b * rows, (b + 1) * rows)
+        turned = by_row(row_tab[0], jnp.concatenate([work[0, at, :], work[1, at, :]], axis=1))
+        for part in range(2):
             for n in range(per_block):
                 for c in range(chunks):
                     at = n * piece + c * rc
-                    s1[c, b * per_block + n, part] = turned[at : at + rc]
+                    s1[c, b * per_block + n, part] = turned[
+                        at : at + rc, part * lanes : (part + 1) * lanes
+                    ]
 
     for c in range(chunks):
         r1[c, me] = s1[c, me]
@@ -228,12 +250,16 @@
         for k in range(1, group):
             arrived(r1.at[c, peer(k)], recv1.at[c, peer(k)], k).wait_recv()
 
+        tall = group * 2 * rc
+        turned = by_lane(r1[c].reshape(tall, lanes), lane_tab[0])
+        mid[...] = turned.reshape(group, 2, rc, lanes)
+
         @pl.loop(0, rc // 8)
         def _(n):
             at = pl.ds(pl.multiple_of(n * 8, 8), 8)
             from_piece = pl.ds(pl.multiple_of(c * rc + n * 8, 8), 8)
-            real = [r1[c, g, 0, at, :] for g in range(group)]
-            imag = [r1[c, g, 1, at, :] for g in range(group)]
+            real = [mid[g, 0, at, :] for g in range(group)]
+            imag = [mid[g, 1, at, :] for g in range(group)]
             for bit in range(all_bits):
                 turn = angle(0, 3 if bit < low_bits else 2)
                 real = rotate_list(real, bit, *turn)
@@ -248,9 +274,11 @@
                 real = rotate_list(real, bit, *turn)
                 imag = rotate_list(imag, bit, *turn)
             for g in range(group):
-                s2[c, g, 0, at, :] = real[g]
-                s2[c, g, 1, at, :] = imag[g]
-
+                mid[g, 0, at, :] = real[g]
+                mid[g, 1, at, :] = imag[g]
+
+        turned = by_lane(mid[...].reshape(tall, lanes), lane_tab[1])
+        s2[c] = turned.reshape(group, 2, rc, lanes)
         r2[c, me] = s2[c, me]
         for k in range(1, group):
             part_copy(s2, r2, send2, recv2, c, k).start()
@@ -258,17 +286,16 @@
     for c in range(chunks):
         for k in range(1, group):
             arrived(r2.at[c, peer(k)], recv2.at[c, peer(k)], k).wait_recv()
-        turned = mm(r2[c].reshape(group * 2 * rc, lanes), lane_tab[1])
-        turned = turned.reshape(group, 2, rc, lanes)
         for g in range(group):
             for part in range(2):
                 at = g * piece + c * rc
-                work[part, at : at + rc, :] = turned[g, part]
-
-    for part in range(2):
-        for b in range(blocks):
-            at = slice(b * rows, (b + 1) * rows)
-            work[part, at, :] = mm(row_tab[1], work[part, at, :])
+                work[part, at : at + rc, :] = r2[c, g, part]
+
+    for b in range(blocks):
+        at = slice(b * rows, (b + 1) * rows)
+        turned = by_row(row_tab[1], jnp.concatenate([work[0, at, :], work[1, at, :]], axis=1))
+        work[0, at, :] = turned[:, :lanes]
+        work[1, at, :] = turned[:, lanes:]
 
     @pl.loop(0, rows // step)
     def _(n):
@@ -307,9 +334,10 @@
         in_specs=[vmem] * 4,
         out_specs=vmem,
         scratch_shapes=[
-            pltpu.VMEM((LAYERS, lanes, lanes), jnp.float32),
-            pltpu.VMEM((LAYERS, rows, rows), jnp.float32),
+            pltpu.VMEM((LAYERS, 2 * lanes, 2 * lanes), jnp.bfloat16),
+            pltpu.VMEM((LAYERS, 2 * rows, 2 * rows), jnp.bfloat16),
             pltpu.VMEM((2, total, lanes), jnp.float32),
+            pltpu.VMEM((group, 2, rc, lanes), jnp.float32),
             parts,
             parts,
             parts,

time: 45.5 us -> 45.3 us (level)
  no operation moved by 1% of the time
where the time goes in v2:
time: 45.3 us; the launch traced here: 45.1 us
  Pallas kernels  43.2 us (95%)
  local copies, waits for them, and re-layouts  1.87 us (4%)
    pallas_call x1, Pallas kernels, body(): pl.pallas_call(functools.partial(kernel, n_high, n_low, blocks, rows, chu...  43.2 us
    unnamed x1, local copies, waits for them, and re-layouts  1.87 us

profile of v2, /device:TPU:0, one launch (start us, length us, event | category | flops | bytes accessed | tf_op | source)
XLA Modules:
  0.0 45.1 jit_solution(7990817565648786433)
XLA Ops:
  0.0 43.2 %shard_map.46 = f32[2,512,128]{2,1,0:T(8,128)} custom-call(f32[2,512,128]{2,1,0:T(8,128)} %bitcast.4, f32[512,128]{1,0:T(8,128)} %bitcast.5, f32[2,128]{1,0:T(2,128)} %phase.1, f32[2,4]{1,0:T(2,128)} %mix.1), custom_call_target="tpu_custom_call" | custom-call | tf_op jit(solution)/shard_map/pallas_call | solution.py:331
  43.2 1.9 %copy.6 = f32[2,4,128,128]{3,2,1,0:T(8,128)} copy(f32[2,4,128,128]{3,2,1,0:T(8,128)} %bitcast.3) | data formatting | bytes 1048576

commit v3 on v2

--- a/solution.py
+++ b/solution.py
@@ -10,7 +10,7 @@
 
 LAYERS = 2
 MESH = pl.DeviceIdType.MESH
-CHUNKS = 4
+CHUNKS = 2
 
 
 def cos_sin(x):

time: 45.3 us -> 41.4 us (0.914)
  Pallas kernels: 43.2 us -> 39.3 us
    pallas_call x1, Pallas kernels: 43.2 us -> 39.3 us  [body(): pl.pallas_call(functools.partial(kernel, n_high, n_low, blocks, rows, chu...]
where the time goes in v3:
time: 41.4 us; the launch traced here: 41.2 us
  Pallas kernels  39.3 us (95%)
  local copies, waits for them, and re-layouts  1.87 us (5%)
    pallas_call x1, Pallas kernels, body(): pl.pallas_call(functools.partial(kernel, n_high, n_low, blocks, rows, chu...  39.3 us
    unnamed x1, local copies, waits for them, and re-layouts  1.87 us

profile of v3, /device:TPU:0, one launch (start us, length us, event | category | flops | bytes accessed | tf_op | source)
XLA Modules:
  0.0 41.2 jit_solution(16531300748632635016)
XLA Ops:
  0.0 39.3 %shard_map.46 = f32[2,512,128]{2,1,0:T(8,128)} custom-call(f32[2,512,128]{2,1,0:T(8,128)} %bitcast.4, f32[512,128]{1,0:T(8,128)} %bitcast.5, f32[2,128]{1,0:T(2,128)} %phase.1, f32[2,4]{1,0:T(2,128)} %mix.1), custom_call_target="tpu_custom_call" | custom-call | tf_op jit(solution)/shard_map/pallas_call | solution.py:331
  39.3 1.9 %copy.6 = f32[2,4,128,128]{3,2,1,0:T(8,128)} copy(f32[2,4,128,128]{3,2,1,0:T(8,128)} %bitcast.3) | data formatting | bytes 1048576
